TPU v7x, 32 devices: a whole 2x2x4 slice. The times are simulated.
32 devices in a mesh: dp: 2 (over core), seq: 4 (over y, x), tensor: 4 (over z).
Axes of the slice: x: 2, y: 2, z: 4, core: 2. Of those that a mesh axis runs over, the one named last changes fastest.
Arguments:
- tokens: bfloat16 [2, 2048, 2048], P('dp', ('seq', 'tensor')), may hold values from -6 to 6
- attn_gain: float32 [2048], replicated, may hold values from 0.5 to 1.5
- w_qkv: bfloat16 [3, 2048, 2048], P(None, None, 'tensor'), may hold values from -1 to 1
- w_out: bfloat16 [2048, 2048], P('tensor'), may hold values from -0.125 to 0.125
- mlp_gain: float32 [2048], replicated, may hold values from 0.5 to 1.5
- w_up: bfloat16 [2048, 8192], P(None, 'tensor'), may hold values from -0.125 to 0.125
- w_down: bfloat16 [8192, 2048], P('tensor'), may hold values from -0.0625 to 0.0625
- pool_gain: float32 [2048], replicated, may hold values from -8 to 8
- pool_bias: float32 [2048], replicated, may hold values from 0.5 to 5
- value_weight: float32 [2048], replicated, may hold values from -6 to 6
- valid_frames: int32 [2], replicated, may hold values from 4 to 8, as said below
Outputs:
- hidden: bfloat16 [2, 2048, 2048], P('dp', ('seq', 'tensor'))
- frame_values: float32 [2, 8], P('dp', 'seq')
- advantages: float32 [2, 8], P('dp', 'seq')
Inputs may be any that keep to these rules, and one draw needn't show every extreme that they name: `valid_frames`: at least one rollout keeps all 8 frames and at least one keeps 8 // 2 of them.
All inputs are finite; a program needn't handle non-finite values.
Results may differ from a plain program's by a relative error of at most 0.017.
Values may be sent and summed in bfloat16 or wider, within the bound.
A program may use at most 256 MiB of HBM per device.

v0:
```python
import jax
import jax.numpy as jnp
from jax import lax
from jax.sharding import PartitionSpec as P

HEAD_DIM = 128
TOK_FRAME = 256
FR_DEV = 2


def entering_2(value, axis, join, neutral):
    count, mine = (lax.axis_size(axis), lax.axis_index(axis))
    pieces = jax.tree.map(lambda part: lax.all_gather(part, axis), value)
    subtotal = jax.tree.map(
        lambda part, zero: jnp.full_like(part, 0) + jnp.asarray(zero, part.dtype), value, neutral
    )

    def turn(position, subtotal):
        longer = join(subtotal, jax.tree.map(lambda part: part[position], pieces))
        return jax.tree.map(lambda new, old: jnp.where(position < mine, new, old), longer, subtotal)

    return lax.fori_loop(0, count - 1, turn, subtotal)


def rms_norm(values, gain):
    floats = values.astype(jnp.float32)
    square = jnp.mean(floats * floats, axis=-1, keepdims=True)
    return (floats * lax.rsqrt(square + 1e-05) * gain).astype(jnp.bfloat16)


def compose(earlier, later):
    return (earlier[0] * later[0], later[0] * earlier[1] + later[1])


def local(
    tokens,
    attn_gain,
    w_qkv,
    w_out,
    mlp_gain,
    w_up,
    w_down,
    pool_gain,
    pool_bias,
    value_weight,
    valid_frames,
):
    rows = tokens[0]
    row_count = rows.shape[0]
    seq_index = lax.axis_index("seq")
    tensor_index = lax.axis_index("tensor")
    roll_index = lax.axis_index("dp")
    length = valid_frames[roll_index]
    local_heads = w_qkv.shape[2] // HEAD_DIM
    scale = 1.0 / HEAD_DIM**0.5
    block_tokens = lax.all_gather(rows, "tensor", axis=0, tiled=True)
    qkv = jnp.einsum(
        "nd,cde->nce", rms_norm(block_tokens, attn_gain), w_qkv, preferred_element_type=jnp.float32
    ).astype(jnp.bfloat16)
    block = qkv.shape[0]
    query = qkv[:, 0].reshape(block, local_heads, HEAD_DIM)
    query_frame = (seq_index * block + jnp.arange(block, dtype=jnp.int32)) // TOK_FRAME
    peak = jnp.full((local_heads, block), -1e30, jnp.float32)
    key_piece = lax.all_gather(qkv[:, 1], "seq", axis=0, tiled=True)
    value_piece = lax.all_gather(qkv[:, 2], "seq", axis=0, tiled=True)
    width = key_piece.shape[0]
    key_heads = key_piece.reshape(width, local_heads, HEAD_DIM)
    value_heads = value_piece.reshape(width, local_heads, HEAD_DIM)
    scores = (
        jnp.einsum("qhe,khe->hqk", query, key_heads, preferred_element_type=jnp.float32) * scale
    )
    key_frame = jnp.arange(width, dtype=jnp.int32) // TOK_FRAME
    allowed = (key_frame[None, :] <= query_frame[:, None]) & (key_frame[None, :] < length)
    scores = jnp.where(allowed[None], scores, -1e30)
    new_peak = jnp.maximum(peak, jnp.max(scores, axis=-1))
    weights = jnp.where(allowed[None], jnp.exp(scores - new_peak[..., None]), 0.0)
    total = jnp.sum(weights, axis=-1)
    acc = jnp.einsum(
        "hqk,khe->hqe",
        weights.astype(jnp.bfloat16),
        value_heads,
        preferred_element_type=jnp.float32,
    )
    peak, total, acc = (new_peak, total, acc)
    mixed = (
        (acc / total[..., None])
        .transpose(1, 0, 2)
        .reshape(block, local_heads * HEAD_DIM)
        .astype(jnp.bfloat16)
    )
    attn_sum = lax.psum(
        jnp.dot(mixed, w_out, preferred_element_type=jnp.float32).astype(jnp.bfloat16), "tensor"
    ).astype(jnp.float32)
    after_attn = (block_tokens.astype(jnp.float32) + attn_sum).astype(jnp.bfloat16)
    up = jax.nn.gelu(
        jnp.dot(rms_norm(after_attn, mlp_gain), w_up, preferred_element_type=jnp.float32),
        approximate=True,
    ).astype(jnp.bfloat16)
    own_after = lax.dynamic_slice_in_dim(after_attn, tensor_index * row_count, row_count, 0)
    down_sum = lax.psum_scatter(
        jnp.dot(up, w_down, preferred_element_type=jnp.float32).astype(jnp.bfloat16),
        "tensor",
        scatter_dimension=0,
        tiled=True,
    ).astype(jnp.float32)
    hidden = (own_after.astype(jnp.float32) + down_sum).astype(jnp.bfloat16)
    local_frame = (tensor_index * row_count + jnp.arange(row_count, dtype=jnp.int32)) // TOK_FRAME
    selector = (local_frame[None, :] == jnp.arange(FR_DEV, dtype=jnp.int32)[:, None]).astype(
        jnp.bfloat16
    )
    sums = jnp.dot(selector, hidden, preferred_element_type=jnp.float32)
    sums = lax.psum(sums, "tensor")
    gain, offset, head_weight = (pool_gain, pool_bias, value_weight)
    means = sums / TOK_FRAME
    frame_global = seq_index * FR_DEV + jnp.arange(FR_DEV, dtype=jnp.int32)
    valid = frame_global < length
    gate = jax.nn.sigmoid(means * gain + offset)
    decay = jnp.where(valid[:, None], gate, 1.0)
    source = jnp.where(valid[:, None], (1.0 - gate) * means, 0.0)
    agg_decay = jnp.ones_like(means[0])
    agg_source = jnp.zeros_like(means[0])
    for frame in range(FR_DEV):
        agg_decay, agg_source = compose((agg_decay, agg_source), (decay[frame], source[frame]))
    entering = entering_2(
        (agg_decay, agg_source),
        "seq",
        compose,
        (jnp.ones_like(agg_decay), jnp.zeros_like(agg_source)),
    )
    state = entering[1]
    collected = []
    for frame in range(FR_DEV):
        state = decay[frame] * state + source[frame]
        collected.append(jnp.sum(state * head_weight))
    partial_values = jnp.stack(collected)
    values = jnp.where(valid, partial_values, 0.0)
    pick = jnp.sum(jnp.where(frame_global == length - 1, values, 0.0))
    count = jnp.sum(valid_frames).astype(jnp.float32)
    slot = (jnp.arange(lax.axis_size("dp"), dtype=jnp.int32) == roll_index).astype(jnp.float32)
    entries = jnp.stack([pick, jnp.sum(values), jnp.sum(values * values)])
    table = lax.psum(entries[:, None] * slot[None, :], ("dp", "seq"))
    finals, first_sums, second_sums = (table[0], table[1], table[2])
    lengths = valid_frames.astype(jnp.float32)
    mean = jnp.sum(lengths * finals - first_sums) / count
    squares = jnp.sum(lengths * finals * finals - 2.0 * finals * first_sums + second_sums) / count
    variance = squares - mean * mean
    final = jnp.sum(finals * slot)
    gap = jnp.where(valid, final - values, 0.0)
    centered = jnp.where(valid, gap - mean, 0.0)
    advantages = jnp.where(valid, centered * lax.rsqrt(variance + 1e-05), 0.0)
    return (hidden[None], values[None], advantages[None])


def solution(mesh):
    in_specs = (
        P("dp", ("seq", "tensor"), None),
        P(),
        P(None, None, "tensor"),
        P("tensor", None),
        P(),
        P(None, "tensor"),
        P("tensor", None),
        P(),
        P(),
        P(),
        P(),
    )
    out_specs = (P("dp", ("seq", "tensor"), None), P("dp", "seq"), P("dp", "seq"))
    return jax.shard_map(local, mesh=mesh, in_specs=in_specs, out_specs=out_specs, check_vma=False)
```

profile of v0, /device:TPU:1, one launch (start us, length us, event | category | flops | bytes accessed | tf_op | source)
XLA Modules:
  0.0 369.2 jit_solution(14914907635023550377)
XLA Ops:
  7.2 0.0 copy-start
  7.2 0.0 all-gather.9.cloned.1.call-start
  7.2 0.7 all-gather.9.cloned.1.call-update
  7.9 0.0 all-gather.11.cloned.1.call-start
  8.0 49.2 %all-gather.9.cloned.1.call-done = bf16[1,512,2048]{2,1,0:T(8,128)(2,1)} async-done(((bf16[1,128,2048]{2,1,0:T(8,128)(2,1)}), bf16[1,512,2048]{2,1,0:T(8,128)(2,1)}) %all-gather.9.cloned.1.call-update) | async-done | bytes 2097168 | tf_op jit(solution)/shard_map/all_gather | solution.py:56
  57.1 2.1 fusion.17
  59.2 0.0 copy-start.5
  59.2 7.1 %fusion.36 = bf16[512,3,512]{0,2,1:T(8,128)(2,1)S(1)} fusion(bf16[3,2048,512]{2,1,0:T(8,128)(2,1)} %param.15, bf16[1,512,2048]{2,1,0:T(8,128)(2,1)} %all-gather.9.cloned.1.call-done, f32[2048]{0:T(1024)} %param.14, f32[512]{0:T(512)S(1)} %add_rsqrt_fusion.1), kind=kOutput, calls=%fused_computation.46 | convolution fusion | flops 3226206208 | bytes 9971712 | tf_op jit(solution)/shard_map/nd,cde->nce/dot_general | solution.py:57
  66.3 1.2 fusion.70
  67.5 0.0 all-gather.11.cloned.1.call-update
  67.5 0.0 all-gather.13.cloned.1.call-start
  67.6 0.7 dynamic_slice.20
  68.3 0.0 all-gather.13.cloned.1.call-update
  68.3 0.2 all-reduce.2.cloned.1.call-start
  68.5 0.6 broadcast_compare_fusion
  69.2 0.7 compare_and_fusion
  69.9 31.6 %all-gather.11.cloned.1.call-done = bf16[2048,1,512]{0,2,1:T(8,128)(2,1)} async-done(((bf16[512,1,512]{0,2,1:T(8,128)(2,1)}), bf16[2048,1,512]{0,2,1:T(8,128)(2,1)}) %all-gather.11.cloned.1.call-update) | async-done | bytes 2097168 | tf_op jit(solution)/shard_map/all_gather | solution.py:64
  101.6 5.2 %fusion = (f32[4,512]{1,0:T(4,128)S(1)}, f32[4,512,2048]{2,1,0:T(8,128)S(1)}) fusion(pred[512,2048]{1,0:T(8,128)(4,1)S(1)} %compare_and_fusion, bf16[512,4,128]{0,2,1:T(8,128)(2,1)} %bitcast.94, bf16[2048,4,128]{0,2,1:T(8,128)(2,1)} %bitcast.93), kind=kOutput, calls=%fused_computation.5 | convolution fusion | flops 1086322688 | bytes 20455424 | tf_op jit(solution)/shard_map/qhe,khe->hqk/dot_general | solution.py:70
  106.8 6.0 %copy-done.1 = f32[4,512,2048]{2,1,0:T(8,128)} copy-done((f32[4,512,2048]{2,1,0:T(8,128)}, f32[4,512,2048]{2,1,0:T(8,128)S(1)}, u32[]{:S(2)}) %copy-start.1) | copy-done | bytes 16777240
  112.9 5.0 %fusion.1 = f32[4,512]{1,0:T(4,128)S(1)} fusion(f32[4,512,2048]{2,1,0:T(8,128)S(1)} %get-tuple-element.152, f32[4,512]{1,0:T(4,128)S(1)} %broadcast_maximum_fusion, pred[512,2048]{1,0:T(8,128)(4,1)S(1)} %compare_and_fusion), kind=kLoop, calls=%fused_computation.6 | loop fusion | flops 20969472 | bytes 17842176 | tf_op jit(solution)/shard_map/reduce_sum | solution.py:77
  117.9 20.6 %all-gather.13.cloned.1.call-done = bf16[2048,1,512]{0,2,1:T(8,128)(2,1)} async-done(((bf16[512,1,512]{0,2,1:T(8,128)(2,1)}), bf16[2048,1,512]{0,2,1:T(8,128)(2,1)}) %all-gather.13.cloned.1.call-update) | async-done | bytes 2097168 | tf_op jit(solution)/shard_map/all_gather | solution.py:65
  138.5 8.7 %divide_convert_fusion = bf16[512,4,128]{0,2,1:T(8,128)(2,1)S(1)} fusion(bf16[2048,4,128]{0,2,1:T(8,128)(2,1)} %bitcast.104, f32[4,512,2048]{2,1,0:T(8,128)} %copy-done.1, f32[4,512]{1,0:T(4,128)S(1)} %broadcast_maximum_fusion, pred[512,2048]{1,0:T(8,128)(4,1)S(1)} %compare_and_fusion, f32[512,4]{0,1:T(4,128)S(1)} %bitcast.103), kind=kOutput, calls=%fused_computation.49 | convolution fusion | flops 1095237632 | bytes 20463616 | tf_op jit(solution)/shard_map/hqk,khe->hqe/dot_general | solution.py:78
  147.2 2.6 convolution_convert_fusion.1
  149.9 0.0 all-reduce.2.cloned.1.call-update
  149.9 0.3 reduce-scatter.2.cloned.1.call-start
  150.2 85.9 %all-reduce.2.cloned.1.call-done = bf16[512,2048]{1,0:T(8,128)(2,1)} async-done(((bf16[512,2048]{1,0:T(8,128)(2,1)}), bf16[512,2048]{1,0:T(8,128)(2,1)}) %all-reduce.2.cloned.1.call-update) | async-done | bytes 2097168 | tf_op jit(solution)/shard_map/psum | solution.py:91
  236.0 4.5 %fusion.6 = (f32[512]{0:T(512)S(1)}, bf16[512,2048]{1,0:T(8,128)(2,1)}) fusion(bf16[512,2048]{1,0:T(8,128)(2,1)} %all-reduce.2.cloned.1.call-done, bf16[1,512,2048]{2,1,0:T(8,128)(2,1)} %all-gather.9.cloned.1.call-done), kind=kLoop, calls=%fused_computation.16 | loop fusion | flops 7339520 | bytes 6293504 | tf_op jit(solution)/shard_map/reduce_sum | solution.py:27
  240.6 0.0 copy-start.4
  240.6 16.6 %convolution_convert_fusion = bf16[512,2048]{1,0:T(8,128)(2,1)} fusion(bf16[2048,2048]{1,0:T(8,128)(2,1)} %param.19, bf16[2048,2048]{1,0:T(8,128)(2,1)} %param.18, bf16[512,2048]{1,0:T(8,128)(2,1)} %get-tuple-element.139, f32[2048]{0:T(1024)S(1)} %copy-done.6, f32[512]{0:T(512)S(1)} %add_rsqrt_fusion), kind=kOutput, calls=%fused_computation.32 | convolution fusion | flops 8604614656 | bytes 20981760 | tf_op jit(solution)/shard_map/dot_general | solution.py:101
  257.2 0.0 reduce-scatter.2.cloned.1.call-update
  257.2 0.6 reduce_sum.118
  258.5 0.6 fusion.60
  259.2 40.8 %reduce-scatter.2.cloned.1.call-done = bf16[128,2048]{1,0:T(8,128)(2,1)} async-done(((bf16[512,2048]{1,0:T(8,128)(2,1)}), bf16[128,2048]{1,0:T(8,128)(2,1)}) %reduce-scatter.2.cloned.1.call-update) | async-done | bytes 524304 | tf_op jit(solution)/shard_map/reduce_scatter | solution.py:100
  300.0 1.4 fusion.44
  301.4 14.0 %psum.22 = f32[2,2048]{1,0:T(2,128)S(1)} all-reduce(f32[2,2048]{1,0:T(2,128)S(1)} %fusion.44), channel_id=1, replica_groups=mesh['dp'=2,'seq'=4,'tensor'=4] {'tensor'}, use_global_device_ids=true, to_apply=%region_6.7 | all-reduce | flops 4096 | bytes 32768 | tf_op jit(solution)/shard_map/psum | solution.py:112
  315.3 0.1 broadcast_select_fusion
  315.4 0.1 multiply_select_fusion.1
  315.5 5.8 %all-gather.4 = f32[4,1,2048]{2,1,0:T(1,128)S(1)} all-gather(f32[1,1,2048]{2,1,0:T(1,128)S(1)} %get-tuple-element.147), channel_id=1, replica_groups=mesh['dp'=2,'seq'=4,'tensor'=4] {'seq'}, dimensions={0}, use_global_device_ids=true | all-gather | bytes 40960 | tf_op jit(solution)/shard_map/all_gather | solution.py:13
  321.4 6.1 %all-gather.3 = f32[4,1,2048]{2,1,0:T(1,128)S(1)} all-gather(f32[1,1,2048]{2,1,0:T(1,128)S(1)} %get-tuple-element.146), channel_id=1, replica_groups=mesh['dp'=2,'seq'=4,'tensor'=4] {'seq'}, dimensions={0}, use_global_device_ids=true | all-gather | bytes 40960 | tf_op jit(solution)/shard_map/all_gather | solution.py:13
  327.5 0.2 while.14
  327.7 0.6 multiply_reduce_fusion.1
  328.3 2.6 fusion.55
  330.9 2.0 pad_maximum_fusion
  332.9 0.1 broadcast_multiply_fusion.1
  333.5 21.9 %psum.23 = f32[3,2]{1,0:T(4,128)S(1)} all-reduce(f32[3,2]{1,0:T(4,128)S(1)} %broadcast_multiply_fusion.1), channel_id=1, replica_groups=mesh['dp'=2,'seq'=4,'tensor'=4] {'dp','seq'}, use_global_device_ids=true, to_apply=%region_14.15 | all-reduce | flops 6 | bytes 48 | tf_op jit(solution)/shard_map/psum | solution.py:141
  355.4 0.6 fusion.57
  357.4 3.1 multiply_select_fusion.2
  360.5 2.1 fusion.45
  (28 shorter events, 0.2 us)
Async XLA Ops:
  7.2 140.0 %copy-start = (bf16[512,2048]{1,0:T(8,128)(2,1)S(1)}, bf16[512,2048]{1,0:T(8,128)(2,1)}, u32[]{:S(2)}) copy-start(bf16[512,2048]{1,0:T(8,128)(2,1)} %param.16) | copy-start | bytes 6291460
  7.2 50.0 %all-gather.9.cloned.1.call-start = ((), (), s32[]{:S(2)}) async-start(), calls=%async_computation.3 | async-start | bytes 2621440 | tf_op jit(solution)/shard_map/all_gather | solution.py:56
  7.9 93.6 %all-gather.11.cloned.1.call-start = ((), (), s32[]{:S(2)}) async-start(), calls=%async_computation.4 | async-start | bytes 2621440 | tf_op jit(solution)/shard_map/all_gather | solution.py:64
  59.2 8.4 %copy-start.5 = (s32[2]{0:T(128)S(1)}, s32[2]{0:T(128)}, u32[]{:S(2)}) copy-start(s32[2]{0:T(128)} %param.23) | copy-start | bytes 28
  67.5 70.9 %all-gather.13.cloned.1.call-start = ((), (), s32[]{:S(2)}) async-start(), calls=%async_computation.5 | async-start | bytes 2621440 | tf_op jit(solution)/shard_map/all_gather | solution.py:65
  68.3 167.7 %all-reduce.2.cloned.1.call-start = ((), (), s32[]{:S(2)}) async-start(), calls=%async_computation.1 | async-start | bytes 4194304 | tf_op jit(solution)/shard_map/psum | solution.py:91
  106.8 6.1 %copy-start.1 = (f32[4,512,2048]{2,1,0:T(8,128)}, f32[4,512,2048]{2,1,0:T(8,128)S(1)}, u32[]{:S(2)}) copy-start(f32[4,512,2048]{2,1,0:T(8,128)S(1)} %get-tuple-element.152) | copy-start | bytes 50331652
  149.9 90.7 %copy-start.6 = (f32[2048]{0:T(1024)S(1)}, f32[2048]{0:T(1024)}, u32[]{:S(2)}) copy-start(f32[2048]{0:T(1024)} %param.17) | copy-start | bytes 24580
  149.9 150.1 %reduce-scatter.2.cloned.1.call-start = ((), (), s32[]{:S(2)}) async-start(), calls=%async_computation.2 | async-start | bytes 2621440 | tf_op jit(solution)/shard_map/reduce_scatter | solution.py:100
  240.6 18.6 %copy-start.3 = (f32[2048]{0:T(1024)S(1)}, f32[2048]{0:T(1024)}, u32[]{:S(2)}) copy-start(f32[2048]{0:T(1024)} %param.20) | copy-start | bytes 24580
  240.6 74.8 %copy-start.4 = (f32[2048]{0:T(1024)S(1)}, f32[2048]{0:T(1024)}, u32[]{:S(2)}) copy-start(f32[2048]{0:T(1024)} %param.21) | copy-start | bytes 24580
  257.2 70.5 %copy-start.2 = (f32[2048]{0:T(1024)S(1)}, f32[2048]{0:T(1024)}, u32[]{:S(2)}) copy-start(f32[2048]{0:T(1024)} %param.22) | copy-start | bytes 24580
Sparse Core Ops, SparseCore 0:
  9.6 47.5 all-gather.8
  67.7 33.8 all-gather.10
  103.4 35.0 all-gather.12
  150.0 85.9 all-reduce.1
  257.3 42.5 reduce-scatter.1
where the time goes:
time: 370 us; the launch traced here: 369 us
  waiting for transfers between devices  229 us (62%)
  blocking collectives  47.8 us (13%)
  matrix products  41.7 us (11%)
  other arithmetic  25.7 us (7%)
  between operations  16.5 us (4%)
  local copies, waits for them, and re-layouts  7.99 us (2%)
    psum x1, waiting for transfers between devices, local(): lax.psum(jnp.dot(mixed, w_out, preferred_element_type=jnp.float32).astype...  85.9 us
    all_gather x1, waiting for transfers between devices, local(): block_tokens = lax.all_gather(rows, 'tensor', axis=0, tiled=True)  49.2 us
    reduce_scatter x1, waiting for transfers between devices, local(): lax.psum_scatter(jnp.dot(up, w_down, preferred_element_type=jnp.float32)....  40.8 us
    all_gather x1, waiting for transfers between devices, local(): key_piece = lax.all_gather(qkv[:, 1], 'seq', axis=0, tiled=True)  31.6 us
    psum x1, blocking collectives, local(): table = lax.psum(entries[:, None] * slot[None, :], ('dp', 'seq'))  21.9 us
    all_gather x1, waiting for transfers between devices, local(): value_piece = lax.all_gather(qkv[:, 2], 'seq', axis=0, tiled=True)  20.6 us
    dot_general x1, matrix products, local(): jnp.dot(up, w_down, preferred_element_type=jnp.float32).astype(jnp.bfloat16)  16.6 us
    psum x1, blocking collectives, local(): sums = lax.psum(sums, 'tensor')  14 us
  transfers between devices with their start and end apart: 5, of which 5 were waited for; matrix products, arithmetic and copies ran while one was open for 4% of the time, Pallas kernels for 0%

commit v1 on v0

--- a/solution.py
+++ b/solution.py
@@ -138,7 +138,9 @@
     count = jnp.sum(valid_frames).astype(jnp.float32)
     slot = (jnp.arange(lax.axis_size("dp"), dtype=jnp.int32) == roll_index).astype(jnp.float32)
     entries = jnp.stack([pick, jnp.sum(values), jnp.sum(values * values)])
-    table = lax.psum(entries[:, None] * slot[None, :], ("dp", "seq"))
+    table = entries[:, None] * slot[None, :]
+    for over in ("dp", "seq"):
+        table = lax.psum(table, over)
     finals, first_sums, second_sums = (table[0], table[1], table[2])
     lengths = valid_frames.astype(jnp.float32)
     mean = jnp.sum(lengths * finals - first_sums) / count

time: 370 us -> 368 us (level)
  blocking collectives: 47.8 us -> 43.3 us
    psum x1 -> x2, blocking collectives: 21.9 us -> 17.5 us  [local(): table = lax.psum(table, over)]
where the time goes in v1:
time: 368 us; the launch traced here: 365 us
  waiting for transfers between devices  229 us (62%)
  blocking collectives  43.3 us (12%)
  matrix products  41.7 us (11%)
  other arithmetic  25.7 us (7%)
  between operations  16.6 us (5%)
  local copies, waits for them, and re-layouts  7.99 us (2%)
    psum x1, waiting for transfers between devices, local(): lax.psum(jnp.dot(mixed, w_out, preferred_element_type=jnp.float32).astype...  85.9 us
    all_gather x1, waiting for transfers between devices, local(): block_tokens = lax.all_gather(rows, 'tensor', axis=0, tiled=True)  49.2 us
    reduce_scatter x1, waiting for transfers between devices, local(): lax.psum_scatter(jnp.dot(up, w_down, preferred_element_type=jnp.float32)....  41.4 us
    all_gather x1, waiting for transfers between devices, local(): key_piece = lax.all_gather(qkv[:, 1], 'seq', axis=0, tiled=True)  31.6 us
    all_gather x1, waiting for transfers between devices, local(): value_piece = lax.all_gather(qkv[:, 2], 'seq', axis=0, tiled=True)  20.6 us
    psum x2, blocking collectives, local(): table = lax.psum(table, over)  17.5 us
    dot_general x1, matrix products, local(): jnp.dot(up, w_down, preferred_element_type=jnp.float32).astype(jnp.bfloat16)  16.6 us
    psum x1, blocking collectives, local(): sums = lax.psum(sums, 'tensor')  14 us
  transfers between devices with their start and end apart: 5, of which 5 were waited for; matrix products, arithmetic and copies ran while one was open for 4% of the time, Pallas kernels for 0%

profile of v1, /device:TPU:1, one launch (start us, length us, event | category | flops | bytes accessed | tf_op | source)
XLA Modules:
  0.0 365.4 jit_solution(4076076993267411949)
XLA Ops:
  7.2 0.0 copy-start
  7.2 0.0 all-gather.9.cloned.1.call-start
  7.2 0.7 all-gather.9.cloned.1.call-update
  7.9 0.0 all-gather.11.cloned.1.call-start
  8.0 49.2 %all-gather.9.cloned.1.call-done = bf16[1,512,2048]{2,1,0:T(8,128)(2,1)} async-done(((bf16[1,128,2048]{2,1,0:T(8,128)(2,1)}), bf16[1,512,2048]{2,1,0:T(8,128)(2,1)}) %all-gather.9.cloned.1.call-update) | async-done | bytes 2097168 | tf_op jit(solution)/shard_map/all_gather | solution.py:56
  57.1 2.1 fusion.17
  59.2 7.1 %fusion.36 = bf16[512,3,512]{0,2,1:T(8,128)(2,1)S(1)} fusion(bf16[3,2048,512]{2,1,0:T(8,128)(2,1)} %param.15, bf16[1,512,2048]{2,1,0:T(8,128)(2,1)} %all-gather.9.cloned.1.call-done, f32[2048]{0:T(1024)} %param.14, f32[512]{0:T(512)S(1)} %add_rsqrt_fusion.1), kind=kOutput, calls=%fused_computation.46 | convolution fusion | flops 3226206208 | bytes 9971712 | tf_op jit(solution)/shard_map/nd,cde->nce/dot_general | solution.py:57
  66.3 1.2 fusion.70
  67.5 0.0 all-gather.11.cloned.1.call-update
  67.5 0.0 all-gather.13.cloned.1.call-start
  67.6 0.7 dynamic_slice.20
  68.3 0.0 all-gather.13.cloned.1.call-update
  68.3 0.2 all-reduce.2.cloned.1.call-start
  68.5 0.6 broadcast_compare_fusion
  69.2 0.7 compare_and_fusion
  69.9 31.6 %all-gather.11.cloned.1.call-done = bf16[2048,1,512]{0,2,1:T(8,128)(2,1)} async-done(((bf16[512,1,512]{0,2,1:T(8,128)(2,1)}), bf16[2048,1,512]{0,2,1:T(8,128)(2,1)}) %all-gather.11.cloned.1.call-update) | async-done | bytes 2097168 | tf_op jit(solution)/shard_map/all_gather | solution.py:64
  101.6 5.2 %fusion = (f32[4,512]{1,0:T(4,128)S(1)}, f32[4,512,2048]{2,1,0:T(8,128)S(1)}) fusion(pred[512,2048]{1,0:T(8,128)(4,1)S(1)} %compare_and_fusion, bf16[512,4,128]{0,2,1:T(8,128)(2,1)} %bitcast.94, bf16[2048,4,128]{0,2,1:T(8,128)(2,1)} %bitcast.93), kind=kOutput, calls=%fused_computation.5 | convolution fusion | flops 1086322688 | bytes 20455424 | tf_op jit(solution)/shard_map/qhe,khe->hqk/dot_general | solution.py:70
  106.8 6.0 %copy-done.1 = f32[4,512,2048]{2,1,0:T(8,128)} copy-done((f32[4,512,2048]{2,1,0:T(8,128)}, f32[4,512,2048]{2,1,0:T(8,128)S(1)}, u32[]{:S(2)}) %copy-start.1) | copy-done | bytes 16777240
  112.9 5.0 %fusion.1 = f32[4,512]{1,0:T(4,128)S(1)} fusion(f32[4,512,2048]{2,1,0:T(8,128)S(1)} %get-tuple-element.152, f32[4,512]{1,0:T(4,128)S(1)} %broadcast_maximum_fusion, pred[512,2048]{1,0:T(8,128)(4,1)S(1)} %compare_and_fusion), kind=kLoop, calls=%fused_computation.6 | loop fusion | flops 20969472 | bytes 17842176 | tf_op jit(solution)/shard_map/reduce_sum | solution.py:77
  117.9 20.6 %all-gather.13.cloned.1.call-done = bf16[2048,1,512]{0,2,1:T(8,128)(2,1)} async-done(((bf16[512,1,512]{0,2,1:T(8,128)(2,1)}), bf16[2048,1,512]{0,2,1:T(8,128)(2,1)}) %all-gather.13.cloned.1.call-update) | async-done | bytes 2097168 | tf_op jit(solution)/shard_map/all_gather | solution.py:65
  138.5 8.7 %divide_convert_fusion = bf16[512,4,128]{0,2,1:T(8,128)(2,1)S(1)} fusion(bf16[2048,4,128]{0,2,1:T(8,128)(2,1)} %bitcast.104, f32[4,512,2048]{2,1,0:T(8,128)} %copy-done.1, f32[4,512]{1,0:T(4,128)S(1)} %broadcast_maximum_fusion, pred[512,2048]{1,0:T(8,128)(4,1)S(1)} %compare_and_fusion, f32[512,4]{0,1:T(4,128)S(1)} %bitcast.103), kind=kOutput, calls=%fused_computation.49 | convolution fusion | flops 1095237632 | bytes 20463616 | tf_op jit(solution)/shard_map/hqk,khe->hqe/dot_general | solution.py:78
  147.2 2.6 convolution_convert_fusion.1
  149.9 0.0 all-reduce.2.cloned.1.call-update
  149.9 0.3 reduce-scatter.2.cloned.1.call-start
  150.2 85.9 %all-reduce.2.cloned.1.call-done = bf16[512,2048]{1,0:T(8,128)(2,1)} async-done(((bf16[512,2048]{1,0:T(8,128)(2,1)}), bf16[512,2048]{1,0:T(8,128)(2,1)}) %all-reduce.2.cloned.1.call-update) | async-done | bytes 2097168 | tf_op jit(solution)/shard_map/psum | solution.py:91
  236.0 4.5 %fusion.6 = (f32[512]{0:T(512)S(1)}, bf16[512,2048]{1,0:T(8,128)(2,1)}) fusion(bf16[512,2048]{1,0:T(8,128)(2,1)} %all-reduce.2.cloned.1.call-done, bf16[1,512,2048]{2,1,0:T(8,128)(2,1)} %all-gather.9.cloned.1.call-done), kind=kLoop, calls=%fused_computation.16 | loop fusion | flops 7339520 | bytes 6293504 | tf_op jit(solution)/shard_map/reduce_sum | solution.py:27
  240.6 0.0 copy-start.4
  240.6 16.6 %convolution_convert_fusion = bf16[512,2048]{1,0:T(8,128)(2,1)} fusion(bf16[2048,2048]{1,0:T(8,128)(2,1)} %param.19, bf16[2048,2048]{1,0:T(8,128)(2,1)} %param.18, bf16[512,2048]{1,0:T(8,128)(2,1)} %get-tuple-element.139, f32[2048]{0:T(1024)S(1)} %copy-done.6, f32[512]{0:T(512)S(1)} %add_rsqrt_fusion), kind=kOutput, calls=%fused_computation.32 | convolution fusion | flops 8604614656 | bytes 20981760 | tf_op jit(solution)/shard_map/dot_general | solution.py:101
  257.2 0.0 reduce-scatter.2.cloned.1.call-update
  257.9 0.6 fusion.60
  258.5 41.4 %reduce-scatter.2.cloned.1.call-done = bf16[128,2048]{1,0:T(8,128)(2,1)} async-done(((bf16[512,2048]{1,0:T(8,128)(2,1)}), bf16[128,2048]{1,0:T(8,128)(2,1)}) %reduce-scatter.2.cloned.1.call-update) | async-done | bytes 524304 | tf_op jit(solution)/shard_map/reduce_scatter | solution.py:100
  300.0 1.4 fusion.44
  301.4 14.0 %psum.29 = f32[2,2048]{1,0:T(2,128)S(1)} all-reduce(f32[2,2048]{1,0:T(2,128)S(1)} %fusion.44), channel_id=1, replica_groups=mesh['dp'=2,'seq'=4,'tensor'=4] {'tensor'}, use_global_device_ids=true, to_apply=%region_6.7 | all-reduce | flops 4096 | bytes 32768 | tf_op jit(solution)/shard_map/psum | solution.py:112
  315.3 0.1 broadcast_select_fusion
  315.4 0.1 multiply_select_fusion.1
  315.5 5.8 %all-gather.4 = f32[4,1,2048]{2,1,0:T(1,128)S(1)} all-gather(f32[1,1,2048]{2,1,0:T(1,128)S(1)} %get-tuple-element.147), channel_id=1, replica_groups=mesh['dp'=2,'seq'=4,'tensor'=4] {'seq'}, dimensions={0}, use_global_device_ids=true | all-gather | bytes 40960 | tf_op jit(solution)/shard_map/all_gather | solution.py:13
  321.4 6.1 %all-gather.3 = f32[4,1,2048]{2,1,0:T(1,128)S(1)} all-gather(f32[1,1,2048]{2,1,0:T(1,128)S(1)} %get-tuple-element.146), channel_id=1, replica_groups=mesh['dp'=2,'seq'=4,'tensor'=4] {'seq'}, dimensions={0}, use_global_device_ids=true | all-gather | bytes 40960 | tf_op jit(solution)/shard_map/all_gather | solution.py:13
  327.5 0.2 while.14
  327.7 0.6 multiply_reduce_fusion.1
  328.3 2.6 fusion.55
  330.9 2.0 pad_maximum_fusion
  332.9 0.1 broadcast_multiply_fusion.1
  332.9 0.6 reduce_sum.118
  333.6 10.6 %psum.30 = f32[3,2]{1,0:T(4,128)S(1)} all-reduce(f32[3,2]{1,0:T(4,128)S(1)} %broadcast_multiply_fusion.1), channel_id=1, replica_groups=mesh['dp'=2,'seq'=4,'tensor'=4] {'dp'}, use_global_device_ids=true, to_apply=%region_14.15 | all-reduce | flops 6 | bytes 48 | tf_op jit(solution)/shard_map/psum | solution.py:143
  344.8 6.9 %psum.31 = f32[3,2]{1,0:T(4,128)S(1)} all-reduce(f32[3,2]{1,0:T(4,128)S(1)} %psum.30), channel_id=1, replica_groups=mesh['dp'=2,'seq'=4,'tensor'=4] {'seq'}, use_global_device_ids=true, to_apply=%region_15.16 | all-reduce | flops 6 | bytes 48 | tf_op jit(solution)/shard_map/psum | solution.py:143
  351.7 0.6 fusion.57
  353.7 3.1 multiply_select_fusion.2
  356.8 2.1 fusion.45
  (29 shorter events, 0.2 us)
Async XLA Ops:
  7.2 140.0 %copy-start = (bf16[512,2048]{1,0:T(8,128)(2,1)S(1)}, bf16[512,2048]{1,0:T(8,128)(2,1)}, u32[]{:S(2)}) copy-start(bf16[512,2048]{1,0:T(8,128)(2,1)} %param.16) | copy-start | bytes 6291460
  7.2 50.0 %all-gather.9.cloned.1.call-start = ((), (), s32[]{:S(2)}) async-start(), calls=%async_computation.3 | async-start | bytes 2621440 | tf_op jit(solution)/shard_map/all_gather | solution.py:56
  7.9 93.6 %all-gather.11.cloned.1.call-start = ((), (), s32[]{:S(2)}) async-start(), calls=%async_computation.4 | async-start | bytes 2621440 | tf_op jit(solution)/shard_map/all_gather | solution.py:64
  59.2 8.4 %copy-start.5 = (s32[2]{0:T(128)S(1)}, s32[2]{0:T(128)}, u32[]{:S(2)}) copy-start(s32[2]{0:T(128)} %param.23) | copy-start | bytes 28
  67.5 70.9 %all-gather.13.cloned.1.call-start = ((), (), s32[]{:S(2)}) async-start(), calls=%async_computation.5 | async-start | bytes 2621440 | tf_op jit(solution)/shard_map/all_gather | solution.py:65
  68.3 167.7 %all-reduce.2.cloned.1.call-start = ((), (), s32[]{:S(2)}) async-start(), calls=%async_computation.1 | async-start | bytes 4194304 | tf_op jit(solution)/shard_map/psum | solution.py:91
  106.8 6.1 %copy-start.1 = (f32[4,512,2048]{2,1,0:T(8,128)}, f32[4,512,2048]{2,1,0:T(8,128)S(1)}, u32[]{:S(2)}) copy-start(f32[4,512,2048]{2,1,0:T(8,128)S(1)} %get-tuple-element.152) | copy-start | bytes 50331652
  149.9 90.7 %copy-start.6 = (f32[2048]{0:T(1024)S(1)}, f32[2048]{0:T(1024)}, u32[]{:S(2)}) copy-start(f32[2048]{0:T(1024)} %param.17) | copy-start | bytes 24580
  149.9 150.1 %reduce-scatter.2.cloned.1.call-start = ((), (), s32[]{:S(2)}) async-start(), calls=%async_computation.2 | async-start | bytes 2621440 | tf_op jit(solution)/shard_map/reduce_scatter | solution.py:100
  240.6 17.9 %copy-start.3 = (f32[2048]{0:T(1024)S(1)}, f32[2048]{0:T(1024)}, u32[]{:S(2)}) copy-start(f32[2048]{0:T(1024)} %param.20) | copy-start | bytes 24580
  240.6 74.8 %copy-start.4 = (f32[2048]{0:T(1024)S(1)}, f32[2048]{0:T(1024)}, u32[]{:S(2)}) copy-start(f32[2048]{0:T(1024)} %param.21) | copy-start | bytes 24580
  257.2 70.5 %copy-start.2 = (f32[2048]{0:T(1024)S(1)}, f32[2048]{0:T(1024)}, u32[]{:S(2)}) copy-start(f32[2048]{0:T(1024)} %param.22) | copy-start | bytes 24580
Sparse Core Ops, SparseCore 0:
  9.6 47.5 all-gather.8
  67.7 33.8 all-gather.10
  103.4 35.0 all-gather.12
  150.0 85.9 all-reduce.1
  257.3 42.5 reduce-scatter.1
